TPU v7x, 256 devices: a whole 4x4x8 slice. The times are simulated.
256 devices in a mesh: tok: 32 (over z_lo, x, core), blk: 8 (over y, z_hi).
Axes of the slice: x: 4, y: 4, z: 8 (z_hi: 2, z_lo: 4; z = z_hi * 4 + z_lo), core: 2. Of those that a mesh axis runs over, the one named last changes fastest.
Arguments:
- activations: bfloat16 [4096, 7168], P('tok', 'blk'), may hold values from -600 to 600
- signs: float32 [7168], P('blk'), may hold values from -1 to 1, as said below
Outputs:
- hessian: float32 [7168, 7168], P('tok', 'blk')
- incoherence: float32 [7168], P('blk')
- largest_ratio: float32 [], replicated
Inputs may be any that keep to these rules, and one draw needn't show every extreme that they name: `signs`: every entry is -1 or 1.
All inputs are finite; a program needn't handle non-finite values.
Results may differ from a plain program's by a relative error of at most 0.0037.
Values may be sent and summed in bfloat16 or wider, within the bound.
A program may use at most 128 MiB of HBM per device.

v0:
```python
import functools
import math
import jax
import jax.numpy as jnp
from jax import lax
from jax.sharding import Mesh
from jax.sharding import PartitionSpec as P

WALSH = 512
MIX = 14
FEATURES = 7168
BLK = ("blk_0", "blk_1")
TOK = ("tok_0", "tok_1", "tok_2")
TOK_BLK = ("tok_0", "tok_1", "tok_2", "blk_0", "blk_1")
EPS = 1e-06
DAMP = 0.01


def over_axes(value, axes):
    return functools.reduce(lax.psum, axes, value)


def laid_out(pieces, dim):
    pieces = jnp.moveaxis(pieces, 0, dim)
    dims = pieces.shape
    return pieces.reshape(*dims[:dim], dims[dim] * dims[dim + 1], *dims[dim + 2 :])


def from_everyone(value, axis):
    copies = jnp.broadcast_to(value, (lax.axis_size(axis), *value.shape))
    return lax.all_to_all(copies, axis, split_axis=0, concat_axis=0, tiled=True)


def gather_directly(value, axis, dim):
    return laid_out(from_everyone(value, axis), dim)


def over_copies(value, axis):
    everything = from_everyone(value, axis)
    return jnp.max(everything, axis=0)


def walsh_table(length):
    position = jnp.arange(length, dtype=jnp.int32)
    parity = jnp.zeros((length, length), jnp.int32)
    for bit_number in range(length.bit_length() - 1):
        parity = parity + (position[:, None] >> bit_number & 1) * (
            position[None, :] >> bit_number & 1
        )
    return (1 - 2 * (parity % 2)).astype(jnp.float32)


def cosine_table(length):
    rows_idx = jnp.arange(length, dtype=jnp.float32)[:, None]
    columns = jnp.arange(length, dtype=jnp.float32)[None, :]
    table = math.sqrt(2.0 / length) * jnp.cos(math.pi * (columns + 0.5) * rows_idx / length)
    return jnp.where(rows_idx == 0.0, table * math.sqrt(0.5), table)


def contract_tokens(left, right):
    return lax.dot_general(
        left, right, (((0,), (0,)), ((), ())), preferred_element_type=jnp.float32
    )


def per_device(activations, signs):
    tok_rows, block_width = activations.shape
    blocks = lax.axis_size(BLK)
    block_index = lax.axis_index(BLK)
    token_groups = lax.axis_size(TOK)
    token_index = lax.axis_index(TOK)
    local_walsh = WALSH // blocks
    signed = activations * signs.astype(jnp.bfloat16)[None, :]
    local_table = jnp.kron(walsh_table(local_walsh) / math.sqrt(local_walsh), cosine_table(MIX).T)
    partial_mix = jnp.dot(signed.astype(jnp.float32), local_table, precision=lax.Precision.HIGHEST)
    grouped = partial_mix.reshape(blocks, tok_rows // blocks, 1, block_width)
    cross_table = walsh_table(blocks) / math.sqrt(blocks)
    combined = jnp.einsum(
        "rs,xisf->xirf",
        cross_table,
        lax.all_to_all(grouped, BLK, split_axis=0, concat_axis=2, tiled=True),
        precision=lax.Precision.HIGHEST,
    )
    spread = lax.all_to_all(
        combined.astype(jnp.bfloat16), BLK, split_axis=2, concat_axis=0, tiled=True
    )
    rotated = spread.reshape(tok_rows, block_width)
    rotated_wide = rotated.astype(jnp.float32)
    trace_total = over_axes(jnp.sum(rotated_wide * rotated_wide), TOK_BLK)
    row_count = FEATURES // token_groups
    gathered = gather_directly(rotated, BLK, 1)
    gram_block = lax.psum_scatter(
        contract_tokens(gathered, rotated), TOK, scatter_dimension=0, tiled=True
    )
    global_rows = token_index * row_count + jnp.arange(row_count, dtype=jnp.int32)[:, None]
    global_columns = block_index * block_width + jnp.arange(block_width, dtype=jnp.int32)[None, :]
    on_diag = global_rows == global_columns
    local_peaks = jnp.max(jnp.where(on_diag, 0.0, jnp.abs(gram_block)), axis=0)
    column_peak = over_copies(local_peaks, TOK)
    diag_mean = trace_total / FEATURES + EPS
    hessian = gram_block / diag_mean + DAMP * on_diag.astype(jnp.float32)
    incoherence = column_peak / diag_mean
    largest_ratio = over_copies(jnp.max(incoherence), BLK)
    return (hessian, incoherence, largest_ratio)


def solution(mesh):
    split = Mesh(mesh.devices.reshape(4, 4, 2, 4, 2), ("tok_0", "tok_1", "tok_2", "blk_0", "blk_1"))
    return jax.shard_map(
        per_device,
        mesh=split,
        in_specs=(P(TOK, BLK), P(BLK)),
        out_specs=(P(TOK, BLK), P(BLK), P()),
        check_vma=False,
    )
```

profile of v0, /device:TPU:1, one launch (start us, length us, event | category | flops | bytes accessed | tf_op | source)
XLA Modules:
  0.0 367.2 jit_solution(6136312836264446147)
XLA Ops:
  7.2 0.1 multiply_select_fusion
  7.3 0.1 fusion.9
  7.5 13.5 %broadcast_multiply_fusion = f32[64,14,64,14]{3,2,1,0:T(8,128)} fusion(f32[14,14]{1,0:T(8,128)S(1)} %multiply_select_fusion, f32[64,64]{1,0:T(8,128)S(1)} %fusion.9), kind=kLoop, calls=%fused_computation | loop fusion | flops 802816 | bytes 3228432 | tf_op jit(solution)/shard_map/jit(kron)/mul | solution.py:74
  21.0 21.0 %reshape.408 = f32[896,896,1]{1,0,2:T(8,128)S(1)} reshape(f32[64,14,64,14]{3,2,1,0:T(8,128)} %broadcast_multiply_fusion) | data formatting | bytes 6422528 | tf_op jit(solution)/shard_map/jit(kron)/mul | solution.py:74
  42.0 0.0 copy-done.1
  42.0 0.0 copy-done
  42.0 2.2 convolution_bitcast_fusion
  44.2 11.6 %all-to-all-start = ((f32[8,16,1,896]{3,1,2,0:T(8,128)}), f32[8,16,1,896]{3,1,2,0:T(8,128)S(1)}, u32[]{:S(2)}, u32[]{:S(2)}) async-start(f32[8,16,1,896]{3,1,2,0:T(8,128)} %convolution_bitcast_fusion), calls=%async_computation | async-start | bytes 917504 | tf_op jit(solution)/shard_map/all_to_all | solution.py:81
  55.8 0.0 reduce-scatter.2.cloned.1.call-start
  55.9 12.6 %all-to-all-done = f32[8,16,1,896]{3,1,2,0:T(8,128)S(1)} async-done(((f32[8,16,1,896]{3,1,2,0:T(8,128)}), f32[8,16,1,896]{3,1,2,0:T(8,128)S(1)}, u32[]{:S(2)}, u32[]{:S(2)}) %all-to-all-start) | async-done | bytes 458784 | tf_op jit(solution)/shard_map/all_to_all | solution.py:81
  68.5 0.6 fusion
  69.1 12.3 %all_to_all.47 = bf16[1,16,8,896]{3,1,0,2:T(8,128)(2,1)S(1)} all-to-all(bf16[1,16,8,896]{3,1,0,2:T(8,128)(2,1)S(1)} %copy.19), channel_id=1, replica_groups=mesh['tok_0'=4,'tok_1'=4,'tok_2'=2,'blk_0'=4,'blk_1'=2] {'blk_0','blk_1'}, dimensions={2} | all-to-all | bytes 458752 | tf_op jit(solution)/shard_map/all_to_all | solution.py:84
  81.4 0.2 copy.20
  81.6 0.2 broadcast_in_dim.15
  81.8 24.9 %all_to_all.48 = bf16[8,128,896]{1,2,0:T(8,128)(2,1)S(1)} all-to-all(bf16[8,128,896]{1,2,0:T(8,128)(2,1)S(1)} %broadcast_in_dim.15), channel_id=1, replica_groups=mesh['tok_0'=4,'tok_1'=4,'tok_2'=2,'blk_0'=4,'blk_1'=2] {'blk_0','blk_1'}, dimensions={0} | all-to-all | bytes 3670016 | tf_op jit(solution)/shard_map/all_to_all | solution.py:31
  106.7 10.3 %fusion.35 = f32[7168,896]{1,0:T(8,128)} fusion(bf16[128,7168]{0,1:T(8,128)(2,1)S(1)} %bitcast.34, bf16[128,896]{1,0:T(8,128)(2,1)S(1)} %bitcast.36), kind=kOutput, calls=%fused_computation.62 | convolution fusion | flops 1644167168 | bytes 27754496 | tf_op jit(solution)/shard_map/dot_general | solution.py:61
  117.0 0.0 reduce-scatter.2.cloned.1.call-update
  117.0 0.7 multiply_reduce_fusion
  117.7 34.7 %psum.35 = f32[]{:T(128)} all-reduce(f32[]{:T(128)} %multiply_reduce_fusion), channel_id=1, replica_groups=mesh['tok_0'=4,'tok_1'=4,'tok_2'=2,'blk_0'=4,'blk_1'=2] {'tok_0'}, use_global_device_ids=true, to_apply=%region_2.3 | all-reduce | flops 1 | bytes 8 | tf_op jit(solution)/shard_map/psum | solution.py:20
  152.4 12.9 %psum.36 = f32[]{:T(128)} all-reduce(f32[]{:T(128)} %psum.35), channel_id=1, replica_groups=mesh['tok_0'=4,'tok_1'=4,'tok_2'=2,'blk_0'=4,'blk_1'=2] {'tok_1'}, use_global_device_ids=true, to_apply=%region_3.4 | all-reduce | flops 1 | bytes 8 | tf_op jit(solution)/shard_map/psum | solution.py:20
  165.4 3.8 %psum.37 = f32[]{:T(128)} all-reduce(f32[]{:T(128)} %psum.36), channel_id=1, replica_groups=mesh['tok_0'=4,'tok_1'=4,'tok_2'=2,'blk_0'=4,'blk_1'=2] {'tok_2'}, use_global_device_ids=true, to_apply=%region_4.5 | all-reduce | flops 1 | bytes 8 | tf_op jit(solution)/shard_map/psum | solution.py:20
  169.1 8.8 %psum.38 = f32[]{:T(128)} all-reduce(f32[]{:T(128)} %psum.37), channel_id=1, replica_groups=mesh['tok_0'=4,'tok_1'=4,'tok_2'=2,'blk_0'=4,'blk_1'=2] {'blk_0'}, use_global_device_ids=true, to_apply=%region_5.6 | all-reduce | flops 1 | bytes 8 | tf_op jit(solution)/shard_map/psum | solution.py:20
  178.0 8.7 %psum.39 = f32[]{:T(128)} all-reduce(f32[]{:T(128)} %psum.38), channel_id=1, replica_groups=mesh['tok_0'=4,'tok_1'=4,'tok_2'=2,'blk_0'=4,'blk_1'=2] {'blk_1'}, use_global_device_ids=true, to_apply=%region_6.7 | all-reduce | flops 1 | bytes 8 | tf_op jit(solution)/shard_map/psum | solution.py:20
  187.3 135.7 %reduce-scatter.2.cloned.1.call-done = f32[224,896]{1,0:T(8,128)} async-done(((f32[7168,896]{1,0:T(8,128)}), f32[224,896]{1,0:T(8,128)}) %reduce-scatter.2.cloned.1.call-update) | async-done | bytes 802832 | tf_op jit(solution)/shard_map/reduce_scatter | solution.py:92
  323.0 2.3 fusion.2
  325.2 0.1 broadcast_in_dim.16
  325.3 16.7 %all_to_all.49 = f32[32,1,896]{2,1,0:T(1,128)S(1)} all-to-all(f32[32,1,896]{2,1,0:T(1,128)S(1)} %broadcast_in_dim.16), channel_id=1, replica_groups=mesh['tok_0'=4,'tok_1'=4,'tok_2'=2,'blk_0'=4,'blk_1'=2] {'tok_0','tok_1'..., dimensions={0} | all-to-all | bytes 229376 | tf_op jit(solution)/shard_map/all_to_all | solution.py:31
  342.0 0.1 reduce_max.37
  342.1 1.2 fusion.34
  343.3 0.6 broadcast_in_dim.17
  343.9 15.8 %all_to_all.50 = f32[8,1,1]{2,1,0:T(1,128)S(1)} all-to-all(f32[8,1,1]{2,1,0:T(1,128)S(1)} %broadcast_in_dim.17), channel_id=1, replica_groups=mesh['tok_0'=4,'tok_1'=4,'tok_2'=2,'blk_0'=4,'blk_1'=2] {'blk_0','blk_1'}, dimensions={0} | all-to-all | bytes 64 | tf_op jit(solution)/shard_map/all_to_all | solution.py:31
  359.8 0.6 reduce_max.39
  (14 shorter events, 0.1 us)
Async XLA Ops:
  21.0 21.0 %copy-start.1 = (f32[896]{0:T(1024)S(1)}, f32[896]{0:T(1024)}, u32[]{:S(2)}) copy-start(f32[896]{0:T(1024)} %param.3) | copy-start | bytes 10756
  21.0 21.0 %copy-start = (bf16[128,896]{1,0:T(8,128)(2,1)S(1)}, bf16[128,896]{1,0:T(8,128)(2,1)}, u32[]{:S(2)}) copy-start(bf16[128,896]{1,0:T(8,128)(2,1)} %param.2) | copy-start | bytes 688132
  44.2 24.3 %all-to-all-start = ((f32[8,16,1,896]{3,1,2,0:T(8,128)}), f32[8,16,1,896]{3,1,2,0:T(8,128)S(1)}, u32[]{:S(2)}, u32[]{:S(2)}) async-start(f32[8,16,1,896]{3,1,2,0:T(8,128)} %convolution_bitcast_fusion), calls=%async_computation | async-start | bytes 917504 | tf_op jit(solution)/shard_map/all_to_all | solution.py:81
  55.8 267.1 %reduce-scatter.2.cloned.1.call-start = ((), (), s32[]{:S(2)}) async-start(), calls=%async_computation.6 | async-start | bytes 26492928 | tf_op jit(solution)/shard_map/reduce_scatter | solution.py:92
Sparse Core Ops, SparseCore 0:
  117.1 205.8 reduce-scatter.1
where the time goes:
time: 368 us; the launch traced here: 367 us
  waiting for transfers between devices  148 us (40%)
  blocking collectives  139 us (38%)
  local copies, waits for them, and re-layouts  22.1 us (6%)
  other arithmetic  18.7 us (5%)
  between operations  14.8 us (4%)
  matrix products  13.1 us (4%)
  starting transfers between devices  11.7 us (3%)
    reduce_scatter x1, waiting for transfers between devices, per_device(): lax.psum_scatter(contract_tokens(gathered, rotated), TOK, scatter_dimensi...  136 us
    psum x5, blocking collectives, over_axes(): return functools.reduce(lax.psum, axes, value)  69 us
    all_to_all x3, blocking collectives, from_everyone(): return lax.all_to_all(copies, axis, split_axis=0, concat_axis=0, tiled=True)  57.4 us
    mul x1, local copies, waits for them, and re-layouts, per_device(): jnp.kron(walsh_table(local_walsh) / math.sqrt(local_walsh), cosine_table(...  21 us
    mul x1, other arithmetic, per_device(): jnp.kron(walsh_table(local_walsh) / math.sqrt(local_walsh), cosine_table(...  13.5 us
    all_to_all x1, waiting for transfers between devices, per_device(): lax.all_to_all(grouped, BLK, split_axis=0, concat_axis=2, tiled=True)  12.6 us
    all_to_all x1, blocking collectives, per_device(): lax.all_to_all(combined.astype(jnp.bfloat16), BLK, split_axis=2, concat_a...  12.3 us
    all_to_all x1, starting transfers between devices, per_device(): lax.all_to_all(grouped, BLK, split_axis=0, concat_axis=2, tiled=True)  11.6 us
  transfers between devices with their start and end apart: 2, of which 2 were waited for; matrix products, arithmetic and copies ran while one was open for 0% of the time, Pallas kernels for 0%

commit v1 on v0

--- a/solution.py
+++ b/solution.py
@@ -78,7 +78,10 @@
     combined = jnp.einsum(
         "rs,xisf->xirf",
         cross_table,
-        lax.all_to_all(grouped, BLK, split_axis=0, concat_axis=2, tiled=True),
+        jnp.concatenate(
+            lax.all_to_all(jnp.stack(jnp.split(grouped, lax.axis_size(BLK), axis=0)), BLK, 0, 0),
+            axis=2,
+        ),
         precision=lax.Precision.HIGHEST,
     )
     spread = lax.all_to_all(

time: 368 us -> 372 us (1.011)
  local copies, waits for them, and re-layouts: 22.1 us -> 27.1 us
    unnamed x4 -> x11, local copies, waits for them, and re-layouts: 0.01 us -> 4.39 us
where the time goes in v1:
time: 372 us; the launch traced here: 371 us
  waiting for transfers between devices  148 us (40%)
  blocking collectives  139 us (37%)
  local copies, waits for them, and re-layouts  27.1 us (7%)
  other arithmetic  18.7 us (5%)
  between operations  14.8 us (4%)
  matrix products  12.3 us (3%)
  starting transfers between devices  11.7 us (3%)
    reduce_scatter x1, waiting for transfers between devices, per_device(): lax.psum_scatter(contract_tokens(gathered, rotated), TOK, scatter_dimensi...  135 us
    psum x5, blocking collectives, over_axes(): return functools.reduce(lax.psum, axes, value)  68.9 us
    all_to_all x3, blocking collectives, from_everyone(): return lax.all_to_all(copies, axis, split_axis=0, concat_axis=0, tiled=True)  57.6 us
    mul x1, local copies, waits for them, and re-layouts, per_device(): jnp.kron(walsh_table(local_walsh) / math.sqrt(local_walsh), cosine_table(...  21 us
    mul x1, other arithmetic, per_device(): jnp.kron(walsh_table(local_walsh) / math.sqrt(local_walsh), cosine_table(...  13.5 us
    all_to_all x1, waiting for transfers between devices, per_device(): lax.all_to_all(jnp.stack(jnp.split(grouped, lax.axis_size(BLK), axis=0)),...  12.6 us
    all_to_all x1, blocking collectives, per_device(): lax.all_to_all(combined.astype(jnp.bfloat16), BLK, split_axis=2, concat_a...  12.3 us
    all_to_all x1, starting transfers between devices, per_device(): lax.all_to_all(jnp.stack(jnp.split(grouped, lax.axis_size(BLK), axis=0)),...  11.6 us
  transfers between devices with their start and end apart: 2, of which 2 were waited for; matrix products, arithmetic and copies ran while one was open for 0% of the time, Pallas kernels for 0%

profile of v1, /device:TPU:1, one launch (start us, length us, event | category | flops | bytes accessed | tf_op | source)
XLA Modules:
  0.0 371.4 jit_solution(14656806548572784562)
XLA Ops:
  7.5 13.5 %broadcast_multiply_fusion = f32[64,14,64,14]{3,2,1,0:T(8,128)} fusion(f32[14,14]{1,0:T(8,128)S(1)} %multiply_select_fusion, f32[64,64]{1,0:T(8,128)S(1)} %fusion.19), kind=kLoop, calls=%fused_computation | loop fusion | flops 802816 | bytes 3228432 | tf_op jit(solution)/shard_map/jit(kron)/mul | solution.py:74
  21.0 21.0 %mul.290 = f32[896,896]{1,0:T(8,128)S(1)} reshape(f32[64,14,64,14]{3,2,1,0:T(8,128)} %broadcast_multiply_fusion) | data formatting | bytes 6422528 | tf_op jit(solution)/shard_map/jit(kron)/mul | solution.py:74
  42.0 1.4 fusion.4
  43.4 0.6 fusion.14
  44.1 0.6 fusion.13
  44.7 0.6 fusion.12
  45.3 0.6 fusion.11
  45.9 0.6 fusion.10
  46.6 0.6 fusion.9
  47.2 0.6 fusion.8
  47.8 0.6 fusion.7
  48.4 11.6 %all-to-all-start = ((f32[8,1,16,1,896]{4,2,3,1,0:T(8,128)}), f32[8,1,16,1,896]{4,2,3,1,0:T(8,128)S(1)}, u32[]{:S(2)}, u32[]{:S(2)}) async-start(f32[8,1,16,1,896]{4,2,3,1,0:T(8,128)} %fusion.7), calls=%async_computation | async-start | bytes 917504 | tf_op jit(solution)/shard_map/all_to_all | solution.py:82
  60.1 12.6 %all-to-all-done = f32[8,1,16,1,896]{4,2,3,1,0:T(8,128)S(1)} async-done(((f32[8,1,16,1,896]{4,2,3,1,0:T(8,128)}), f32[8,1,16,1,896]{4,2,3,1,0:T(8,128)S(1)}, u32[]{:S(2)}, u32[]{:S(2)}) %all-to-all-start) | async-done | bytes 458784 | tf_op jit(solution)/shard_map/all_to_all | solution.py:82
  72.7 0.6 fusion
  73.4 12.3 %all_to_all.37 = bf16[1,16,8,896]{3,1,0,2:T(8,128)(2,1)S(1)} all-to-all(bf16[1,16,8,896]{3,1,0,2:T(8,128)(2,1)S(1)} %copy.16), channel_id=1, replica_groups=mesh['tok_0'=4,'tok_1'=4,'tok_2'=2,'blk_0'=4,'blk_1'=2] {'blk_0','blk_1'}, dimensions={2} | all-to-all | bytes 458752 | tf_op jit(solution)/shard_map/all_to_all | solution.py:87
  85.7 0.2 copy.17
  85.8 0.2 broadcast_in_dim.15
  86.1 24.9 %all_to_all.38 = bf16[8,128,896]{1,2,0:T(8,128)(2,1)S(1)} all-to-all(bf16[8,128,896]{1,2,0:T(8,128)(2,1)S(1)} %broadcast_in_dim.15), channel_id=1, replica_groups=mesh['tok_0'=4,'tok_1'=4,'tok_2'=2,'blk_0'=4,'blk_1'=2] {'blk_0','blk_1'}, dimensions={0} | all-to-all | bytes 3670016 | tf_op jit(solution)/shard_map/all_to_all | solution.py:31
  111.0 10.3 %fusion.45 = f32[7168,896]{1,0:T(8,128)} fusion(bf16[128,7168]{0,1:T(8,128)(2,1)S(1)} %bitcast.56, bf16[128,896]{1,0:T(8,128)(2,1)S(1)} %bitcast.58), kind=kOutput, calls=%fused_computation.78 | convolution fusion | flops 1644167168 | bytes 27754496 | tf_op jit(solution)/shard_map/dot_general | solution.py:61
  121.2 0.7 multiply_reduce_fusion
  122.0 34.7 %psum.35 = f32[]{:T(128)} all-reduce(f32[]{:T(128)} %multiply_reduce_fusion), channel_id=1, replica_groups=mesh['tok_0'=4,'tok_1'=4,'tok_2'=2,'blk_0'=4,'blk_1'=2] {'tok_0'}, use_global_device_ids=true, to_apply=%region_2.3 | all-reduce | flops 1 | bytes 8 | tf_op jit(solution)/shard_map/psum | solution.py:20
  156.7 12.9 %psum.36 = f32[]{:T(128)} all-reduce(f32[]{:T(128)} %psum.35), channel_id=1, replica_groups=mesh['tok_0'=4,'tok_1'=4,'tok_2'=2,'blk_0'=4,'blk_1'=2] {'tok_1'}, use_global_device_ids=true, to_apply=%region_3.4 | all-reduce | flops 1 | bytes 8 | tf_op jit(solution)/shard_map/psum | solution.py:20
  169.6 3.8 %psum.37 = f32[]{:T(128)} all-reduce(f32[]{:T(128)} %psum.36), channel_id=1, replica_groups=mesh['tok_0'=4,'tok_1'=4,'tok_2'=2,'blk_0'=4,'blk_1'=2] {'tok_2'}, use_global_device_ids=true, to_apply=%region_4.5 | all-reduce | flops 1 | bytes 8 | tf_op jit(solution)/shard_map/psum | solution.py:20
  173.4 8.8 %psum.38 = f32[]{:T(128)} all-reduce(f32[]{:T(128)} %psum.37), channel_id=1, replica_groups=mesh['tok_0'=4,'tok_1'=4,'tok_2'=2,'blk_0'=4,'blk_1'=2] {'blk_0'}, use_global_device_ids=true, to_apply=%region_5.6 | all-reduce | flops 1 | bytes 8 | tf_op jit(solution)/shard_map/psum | solution.py:20
  182.2 8.7 %psum.39 = f32[]{:T(128)} all-reduce(f32[]{:T(128)} %psum.38), channel_id=1, replica_groups=mesh['tok_0'=4,'tok_1'=4,'tok_2'=2,'blk_0'=4,'blk_1'=2] {'blk_1'}, use_global_device_ids=true, to_apply=%region_6.7 | all-reduce | flops 1 | bytes 8 | tf_op jit(solution)/shard_map/psum | solution.py:20
  191.6 135.4 %reduce-scatter.2.cloned.1.call-done = f32[224,896]{1,0:T(8,128)} async-done(((f32[7168,896]{1,0:T(8,128)}), f32[224,896]{1,0:T(8,128)}) %reduce-scatter.2.cloned.1.call-update) | async-done | bytes 802832 | tf_op jit(solution)/shard_map/reduce_scatter | solution.py:95
  327.0 2.3 fusion.2
  329.3 16.7 %all_to_all.39 = f32[32,1,896]{2,1,0:T(1,128)S(1)} all-to-all(f32[32,1,896]{2,1,0:T(1,128)S(1)} %broadcast_in_dim.16), channel_id=1, replica_groups=mesh['tok_0'=4,'tok_1'=4,'tok_2'=2,'blk_0'=4,'blk_1'=2] {'tok_0','tok_1'..., dimensions={0} | all-to-all | bytes 229376 | tf_op jit(solution)/shard_map/all_to_all | solution.py:31
  346.0 1.2 fusion.44
  347.2 0.6 broadcast_in_dim.17
  347.9 16.1 %all_to_all.40 = f32[8,1,1]{2,1,0:T(1,128)S(1)} all-to-all(f32[8,1,1]{2,1,0:T(1,128)S(1)} %broadcast_in_dim.17), channel_id=1, replica_groups=mesh['tok_0'=4,'tok_1'=4,'tok_2'=2,'blk_0'=4,'blk_1'=2] {'blk_0','blk_1'}, dimensions={0} | all-to-all | bytes 64 | tf_op jit(solution)/shard_map/all_to_all | solution.py:31
  364.0 0.6 reduce_max.39
  (21 shorter events, 0.5 us)
Async XLA Ops:
  21.0 21.0 %copy-start.1 = (f32[896]{0:T(1024)S(1)}, f32[896]{0:T(1024)}, u32[]{:S(2)}) copy-start(f32[896]{0:T(1024)} %param.3) | copy-start | bytes 10756
  21.0 21.0 %copy-start = (bf16[128,896]{1,0:T(8,128)(2,1)S(1)}, bf16[128,896]{1,0:T(8,128)(2,1)}, u32[]{:S(2)}) copy-start(bf16[128,896]{1,0:T(8,128)(2,1)} %param.2) | copy-start | bytes 688132
  48.4 24.3 %all-to-all-start = ((f32[8,1,16,1,896]{4,2,3,1,0:T(8,128)}), f32[8,1,16,1,896]{4,2,3,1,0:T(8,128)S(1)}, u32[]{:S(2)}, u32[]{:S(2)}) async-start(f32[8,1,16,1,896]{4,2,3,1,0:T(8,128)} %fusion.7), calls=%async_computation | async-start | bytes 917504 | tf_op jit(solution)/shard_map/all_to_all | solution.py:82
  60.1 266.9 %reduce-scatter.2.cloned.1.call-start = ((), (), s32[]{:S(2)}) async-start(), calls=%async_computation.6 | async-start | bytes 26492928 | tf_op jit(solution)/shard_map/reduce_scatter | solution.py:95
Sparse Core Ops, SparseCore 0:
  121.3 205.5 reduce-scatter.1
